TPU v7x, 32 devices: a whole 2x2x4 slice. The times are simulated.
32 devices in a mesh: patch: 16 (over z, y, core), band: 2 (over x).
Axes of the slice: x: 2, y: 2, z: 4, core: 2. Of those that a mesh axis runs over, the one named last changes fastest.
Arguments:
- latents: float32 [10240, 512], P('patch', 'band'), may hold values from -6 to 6
- edge_latents: float32 [81920, 512], P(('patch', 'band')), may hold values from -6 to 6
- edge_sender: int32 [81920], P(('patch', 'band')), may hold values from 0 to 575, as said below
- edge_receiver: int32 [81920], P(('patch', 'band')), may hold values from 0 to 319
- block_counts: int32 [640], P(('patch', 'band')), may hold values from 16 to 128, as said below
- send_rows: int32 [32, 32, 8], P(('patch', 'band')), may hold values from 0 to 319
- edge_first_weight: bfloat16 [2, 1536, 512], replicated, may hold values from -0.15625 to 0.15625
- edge_first_bias: float32 [2, 512], replicated, may hold values from -3 to 3
- edge_second_weight: bfloat16 [2, 512, 512], replicated
- edge_gain: float32 [2, 512], replicated, may hold values from 0.1 to 1.9
- edge_offset: float32 [2, 512], replicated, may hold values from -3 to 3
- node_first_weight: bfloat16 [2, 1024, 512], replicated, may hold values from -0.1875 to 0.1875
- node_first_bias: float32 [2, 512], replicated, may hold values from -3 to 3
- node_second_weight: bfloat16 [2, 512, 512], replicated
- node_gain: float32 [2, 512], replicated, may hold values from 0.1 to 1.9
- node_offset: float32 [2, 512], replicated, may hold values from -3 to 3
Outputs:
- new_nodes: float32 [10240, 512], P(('patch', 'band'))
- new_edges: float32 [81920, 512], P(('patch', 'band'))
Inputs may be any that keep to these rules, and one draw needn't show every extreme that they name: `edge_sender`: an entry below 320 names a node row of the edge's own device; an entry k above names slot (k - 320) % 8 of the rows that device (k - 320) // 8 sends to the edge's device. `block_counts`: the used slots of a block are its first ones; every device has a full block. send_rows[d, q] lists node rows of device d, numbered within d, that device q receives from d.
All inputs are finite; a program needn't handle non-finite values.
Results may differ from a plain program's by a relative error of at most 0.0045.
Values may be sent and summed in bfloat16 or wider, within the bound.
No kernel may reach another device: no remote copies, remote signals or barrier semaphores. Data moves between devices by JAX's collectives and lax.ppermute only.
A program may use at most 128 MiB of HBM per device.

v0:
```python
import jax
import jax.numpy as jnp
from jax import lax
from jax.sharding import PartitionSpec as P

epsilon = 1e-05


def layer_norm(values, norm_gain, norm_offset):
    centre = values - jnp.mean(values, axis=-1, keepdims=True)
    spread = jnp.mean(centre * centre, axis=-1, keepdims=True)
    return centre * lax.rsqrt(spread + epsilon) * norm_gain + norm_offset


def perceptron(pieces, first_weight, first_bias, second_weight, norm_gain, norm_offset):
    columns = pieces[0].shape[1]
    running = first_bias
    for position in range(len(pieces)):
        running = running + jnp.dot(
            pieces[position],
            first_weight[position * columns : (position + 1) * columns],
            preferred_element_type=jnp.float32,
        )
    active = (running * jax.nn.sigmoid(running)).astype(jnp.bfloat16)
    result = jnp.dot(active, second_weight, preferred_element_type=jnp.float32)
    return layer_norm(result, norm_gain, norm_offset)


def fetch_halo(node_low, send_lists):
    outgoing = node_low[send_lists]
    return lax.all_to_all(outgoing, ("patch", "band"), split_axis=0, concat_axis=0, tiled=True)


def shards(
    latents,
    edge_latents,
    edge_sender,
    edge_receiver,
    block_counts,
    send_rows,
    edge_first_weight,
    edge_first_bias,
    edge_second_weight,
    edge_gain,
    edge_offset,
    node_first_weight,
    node_first_bias,
    node_second_weight,
    node_gain,
    node_offset,
):
    layers = edge_first_weight.shape[0]
    send_lists = send_rows[0]
    block_length = edge_sender.shape[0] // block_counts.shape[0]
    usable = (jnp.arange(block_length, dtype=jnp.int32)[None, :] < block_counts[:, None]).reshape(
        -1
    )
    first_rows = None
    node_state = lax.all_to_all(latents, "band", split_axis=0, concat_axis=1, tiled=True)
    edge_state = edge_latents
    node_count = node_state.shape[0]
    matches = jnp.arange(node_count, dtype=jnp.int32)[:, None] == edge_receiver[None, :]
    receiver_hot = matches.astype(jnp.bfloat16)
    summing_hot = (matches & usable[None, :]).astype(jnp.bfloat16)
    for layer_index in range(layers):
        node_low = node_state.astype(jnp.bfloat16)
        incoming = fetch_halo(node_low, send_lists)
        sender_table = jnp.concatenate([node_low, incoming.reshape(-1, node_low.shape[1])], axis=0)
        receiver_rows = lax.dot_general(
            receiver_hot, node_low, (((0,), (0,)), ((), ())), preferred_element_type=jnp.float32
        ).astype(jnp.bfloat16)
        edge_low = edge_state.astype(jnp.bfloat16)
        update = perceptron(
            (edge_low, sender_table[edge_sender], receiver_rows),
            edge_first_weight[layer_index],
            edge_first_bias[layer_index],
            edge_second_weight[layer_index],
            edge_gain[layer_index],
            edge_offset[layer_index],
        )
        edge_state = edge_state + jnp.where(usable[:, None], update, jnp.zeros_like(update))
        edge_out_low = edge_state.astype(jnp.bfloat16)
        summed = jnp.dot(summing_hot, edge_out_low, preferred_element_type=jnp.float32)
        summed_low = summed.astype(jnp.bfloat16)
        node_state = node_state + perceptron(
            (node_low, summed_low),
            node_first_weight[layer_index],
            node_first_bias[layer_index],
            node_second_weight[layer_index],
            node_gain[layer_index],
            node_offset[layer_index],
        )
    return (node_state, edge_state)


def solution(mesh):
    return jax.shard_map(
        shards,
        mesh=mesh,
        in_specs=(
            P("patch", "band"),
            P(("patch", "band"), None),
            P(("patch", "band")),
            P(("patch", "band")),
            P(("patch", "band")),
            P(("patch", "band"), None, None),
            P(),
            P(),
            P(),
            P(),
            P(),
            P(),
            P(),
            P(),
            P(),
            P(),
        ),
        out_specs=(P(("patch", "band"), None), P(("patch", "band"), None)),
        check_vma=False,
    )
```

profile of v0, /device:TPU:0, one launch (start us, length us, event | category | flops | bytes accessed | tf_op | source)
XLA Modules:
  0.0 148.7 jit_solution(3055805901451270836)
XLA Ops:
  0.6 4.2 %all-to-all-start = ((f32[2,320,256]{2,1,0:T(8,128)}), f32[2,320,256]{2,1,0:T(8,128)S(1)}, u32[]{:S(2)}, u32[]{:S(2)}) async-start(f32[2,320,256]{2,1,0:T(8,128)} %bitcast.105), calls=%async_computation | async-start | bytes 1310720 | tf_op jit(solution)/shard_map/all_to_all | solution.py:59
  7.8 5.9 %copy.32 = f32[2560,512]{0,1:T(8,128)} copy(f32[2560,512]{1,0:T(8,128)} %param.17) | data formatting | bytes 10485760 | tf_op args[1]
  13.7 6.5 %fusion.6 = f32[2560,512]{1,0:T(8,128)} fusion(f32[2560,512]{1,0:T(8,128)} %param.17, bf16[2,1536,512]{2,1,0:T(8,128)(2,1)} %param.22), kind=kOutput, calls=%fused_computation.17 | convolution fusion | flops 1343488000 | bytes 11010048 | tf_op jit(solution)/shard_map/dot_general | solution.py:19
  26.7 7.1 %all-to-all-start.1 = ((bf16[32,8,512]{2,1,0:T(8,128)(2,1)}), bf16[32,8,512]{2,1,0:T(8,128)(2,1)S(1)}, u32[]{:S(2)}, u32[]{:S(2)}) async-start(bf16[32,8,512]{2,1,0:T(8,128)(2,1)} %bitcast.8), calls=%async_computation.1 | async-start | bytes 524288 | tf_op jit(solution)/shard_map/all_to_all | solution.py:31
  33.9 2.2 %convolution_add_fusion.3 = f32[320,512]{1,0:T(8,128)} fusion(bf16[320,512]{1,0:T(8,128)(2,1)S(1)} %bitcast.102, bf16[2,1024,512]{2,1,0:T(8,128)(2,1)} %param.27, f32[512]{0:T(512)S(1)} %bitcast.113), kind=kOutput, calls=%fused_computation.33 | convolution fusion | flops 167936000 | bytes 1509376 | tf_op jit(solution)/shard_map/dot_general | solution.py:19
  36.2 3.1 %convolution_convert_fusion.1 = bf16[2560,512]{1,0:T(8,128)(2,1)} fusion(bf16[320,512]{1,0:T(8,128)(2,1)S(1)} %convert_element_type.50, s32[2560]{0:T(1024)S(1)} %copy-done.36), kind=kOutput, calls=%fused_computation.11 | convolution fusion | flops 840990720 | bytes 2959360 | tf_op jit(solution)/shard_map/dot_general | solution.py:69
  39.2 5.3 %all-to-all-done.1 = bf16[32,8,512]{2,1,0:T(8,128)(2,1)S(1)} async-done(((bf16[32,8,512]{2,1,0:T(8,128)(2,1)}), bf16[32,8,512]{2,1,0:T(8,128)(2,1)S(1)}, u32[]{:S(2)}, u32[]{:S(2)}) %all-to-all-start.1) | async-done | bytes 262176 | tf_op jit(solution)/shard_map/all_to_all | solution.py:31
  44.6 7.8 %gather_fusion.1 = bf16[2560,512]{1,0:T(8,128)(2,1)S(1)} fusion(bf16[576,512]{1,0:T(8,128)(2,1)S(1)} %pad_maximum_fusion, s32[3072]{0:T(1024)S(1)} %pad_clamp_fusion), kind=kCustom, calls=%fused_computation.1 | custom fusion | bytes 5253120 | tf_op jit(solution)/shard_map/gather | solution.py:74
  52.4 4.9 %fusion.61 = f32[2560,512]{1,0:T(8,128)} fusion(bf16[2560,512]{1,0:T(8,128)(2,1)S(1)} %gather_fusion.1, bf16[2,1536,512]{2,1,0:T(8,128)(2,1)} %param.22), kind=kOutput, calls=%fused_computation.59 | convolution fusion | flops 1342177280 | bytes 8388608 | tf_op jit(solution)/shard_map/dot_general | solution.py:19
  57.4 11.1 %fusion.92 = (f32[2560]{0:T(1024)S(1)}, f32[2560,512]{0,1:T(8,128)}) fusion(bf16[2,512,512]{2,1,0:T(8,128)(2,1)} %param.24, f32[2560,512]{1,0:T(8,128)} %fusion.61, f32[2560,512]{1,0:T(8,128)} %fusion.6, bf16[2560,512]{1,0:T(8,128)(2,1)} %convolution_convert_fusion.1, f32[512]{0:T(512)S(1)} %bitcast.119, bf16[2,1536,512]{2,1,0:T(8,128)(2,1)} %param.22), kind=kOutput, calls=%fused_computation.101 | convolution fusion | flops 2696148480 | bytes 19410944 | tf_op jit(solution)/shard_map/dot_general | solution.py:25
  68.4 3.2 %multiply_reduce_fusion.1 = f32[2560]{0:T(1024)S(1)} fusion(f32[2560,512]{0,1:T(8,128)} %get-tuple-element.23, f32[2560]{0:T(1024)S(1)} %broadcast_multiply_fusion.1), kind=kLoop, calls=%fused_computation.8 | loop fusion | flops 3929600 | bytes 5263360 | tf_op jit(solution)/shard_map/reduce_sum | solution.py:11
  72.5 6.3 %select_add_fusion.1 = f32[2560,512]{0,1:T(8,128)} fusion(f32[2560,512]{0,1:T(8,128)} %copy.32, f32[2560,512]{0,1:T(8,128)S(1)} %copy-done.1, f32[512]{0:T(512)S(1)} %bitcast.117, f32[512]{0:T(512)S(1)} %bitcast.116, f32[2560]{0:T(1024)S(1)} %add_rsqrt_fusion.1, f32[2560]{0:T(1024)S(1)} %broadcast_multiply_fusion.1, pred[2560]{0:T(1024)(128)(4,1)S(1)} %copy-done.13), kind=kLoop, calls=%fused_computation.7 | loop fusion | flops 7864320 | bytes 15755776 | tf_op jit(solution)/shard_map/add | solution.py:81
  78.8 4.1 %multiply_convert_fusion.3 = bf16[320,512]{1,0:T(8,128)(2,1)S(1)} fusion(f32[320,512]{1,0:T(8,128)S(1)} %copy-done.10, f32[2560,512]{0,1:T(8,128)} %select_add_fusion.1, s32[2560]{0:T(1024)S(1)} %copy-done.37, pred[2560]{0:T(1024)(128)(4,1)S(1)} %copy-done.13, bf16[2,1024,512]{2,1,0:T(8,128)(2,1)} %param.27), kind=kOutput, calls=%fused_computation.42 | convolution fusion | flops 1010728960 | bytes 6763008 | tf_op jit(solution)/shard_map/dot_general | solution.py:19
  86.3 3.1 %convolution_convert_fusion = bf16[2560,512]{1,0:T(8,128)(2,1)} fusion(bf16[320,512]{1,0:T(8,128)(2,1)S(1)} %fusion.85, s32[2560]{0:T(1024)S(1)} %copy-done.37), kind=kOutput, calls=%fused_computation.10 | convolution fusion | flops 840990720 | bytes 2959360 | tf_op jit(solution)/shard_map/dot_general | solution.py:69
  89.4 2.8 %all-to-all-start.2 = ((bf16[32,8,512]{2,1,0:T(8,128)(2,1)}), bf16[32,8,512]{2,1,0:T(8,128)(2,1)S(1)}, u32[]{:S(2)}, u32[]{:S(2)}) async-start(bf16[32,8,512]{2,1,0:T(8,128)(2,1)} %bitcast.23), calls=%async_computation.2 | async-start | bytes 524288 | tf_op jit(solution)/shard_map/all_to_all | solution.py:31
  92.2 2.2 %convolution_add_fusion.1 = f32[320,512]{1,0:T(8,128)} fusion(bf16[320,512]{1,0:T(8,128)(2,1)S(1)} %fusion.85, bf16[2,1024,512]{2,1,0:T(8,128)(2,1)} %param.27, f32[512]{0:T(512)S(1)} %bitcast.112), kind=kOutput, calls=%fused_computation.31 | convolution fusion | flops 167936000 | bytes 1509376 | tf_op jit(solution)/shard_map/dot_general | solution.py:19
  94.4 6.5 %fusion.16 = f32[2560,512]{1,0:T(8,128)} fusion(f32[2560,512]{0,1:T(8,128)} %select_add_fusion.1, bf16[2,1536,512]{2,1,0:T(8,128)(2,1)} %param.22), kind=kOutput, calls=%fused_computation.27 | convolution fusion | flops 1343488000 | bytes 11010048 | tf_op jit(solution)/shard_map/dot_general | solution.py:19
  102.7 7.7 %gather_fusion.3 = bf16[2560,512]{1,0:T(8,128)(2,1)S(1)} fusion(bf16[576,512]{1,0:T(8,128)(2,1)S(1)} %pad_maximum_fusion.1, s32[3072]{0:T(1024)S(1)} %pad_clamp_fusion), kind=kCustom, calls=%fused_computation.3 | custom fusion | bytes 5253120 | tf_op jit(solution)/shard_map/gather | solution.py:74
  110.4 4.9 %fusion.51 = f32[2560,512]{1,0:T(8,128)} fusion(bf16[2560,512]{1,0:T(8,128)(2,1)S(1)} %gather_fusion.3, bf16[2,1536,512]{2,1,0:T(8,128)(2,1)} %param.22), kind=kOutput, calls=%fused_computation.50 | convolution fusion | flops 1342177280 | bytes 8388608 | tf_op jit(solution)/shard_map/dot_general | solution.py:19
  115.3 11.1 %fusion.96 = (f32[2560]{0:T(1024)S(1)}, f32[2560,512]{0,1:T(8,128)}) fusion(bf16[2,512,512]{2,1,0:T(8,128)(2,1)} %param.24, f32[2560,512]{1,0:T(8,128)} %fusion.51, f32[2560,512]{1,0:T(8,128)} %fusion.16, bf16[2560,512]{1,0:T(8,128)(2,1)} %convolution_convert_fusion, f32[512]{0:T(512)S(1)} %bitcast.118, bf16[2,1536,512]{2,1,0:T(8,128)(2,1)} %param.22), kind=kOutput, calls=%fused_computation.103 | convolution fusion | flops 2696148480 | bytes 19410944 | tf_op jit(solution)/shard_map/dot_general | solution.py:25
  126.4 3.2 %multiply_reduce_fusion = f32[2560]{0:T(1024)S(1)} fusion(f32[2560,512]{0,1:T(8,128)} %get-tuple-element.27, f32[2560]{0:T(1024)S(1)} %broadcast_multiply_fusion), kind=kLoop, calls=%fused_computation.5 | loop fusion | flops 3929600 | bytes 5263360 | tf_op jit(solution)/shard_map/reduce_sum | solution.py:11
  130.4 6.2 %select_add_fusion = f32[2560,512]{0,1:T(8,128)} fusion(f32[2560,512]{0,1:T(8,128)} %select_add_fusion.1, f32[2560,512]{0,1:T(8,128)S(1)} %copy-done, f32[512]{0:T(512)S(1)} %bitcast.115, f32[512]{0:T(512)S(1)} %bitcast.114, f32[2560]{0:T(1024)S(1)} %add_rsqrt_fusion, f32[2560]{0:T(1024)S(1)} %broadcast_multiply_fusion, pred[2560]{0:T(1024)(128)(4,1)S(1)} %copy-done.14), kind=kLoop, calls=%fused_computation.4 | loop fusion | flops 7864320 | bytes 15755776 | tf_op jit(solution)/shard_map/add | solution.py:81
  136.6 5.9 %copy.33 = f32[2560,512]{1,0:T(8,128)} copy(f32[2560,512]{0,1:T(8,128)} %select_add_fusion) | data formatting | bytes 10485760
  142.7 4.1 %multiply_convert_fusion.2 = bf16[320,512]{1,0:T(8,128)(2,1)S(1)} fusion(f32[320,512]{1,0:T(8,128)S(1)} %copy-done.9, f32[2560,512]{0,1:T(8,128)} %select_add_fusion, s32[2560]{0:T(1024)S(1)} %copy-done.38, pred[2560]{0:T(1024)(128)(4,1)S(1)} %copy-done.14, bf16[2,1024,512]{2,1,0:T(8,128)(2,1)} %param.27), kind=kOutput, calls=%fused_computation.39 | convolution fusion | flops 1010728960 | bytes 6763008 | tf_op jit(solution)/shard_map/dot_general | solution.py:19
  (115 shorter events, 18.1 us)
Async XLA Ops:
  0.6 23.3 %all-to-all-start = ((f32[2,320,256]{2,1,0:T(8,128)}), f32[2,320,256]{2,1,0:T(8,128)S(1)}, u32[]{:S(2)}, u32[]{:S(2)}) async-start(f32[2,320,256]{2,1,0:T(8,128)} %bitcast.105), calls=%async_computation | async-start | bytes 1310720 | tf_op jit(solution)/shard_map/all_to_all | solution.py:59
  13.7 6.5 %copy-start.35 = (s32[20]{0:T(128)S(1)}, s32[20]{0:T(128)}, u32[]{:S(2)}) copy-start(s32[20]{0:T(128)} %param.20) | copy-start | bytes 244
  13.7 7.2 %copy-start.28 = (f32[2,512]{1,0:T(2,128)S(1)}, f32[2,512]{1,0:T(2,128)}, u32[]{:S(2)}) copy-start(f32[2,512]{1,0:T(2,128)} %param.25) | copy-start | bytes 12292
  13.7 7.8 %copy-start.29 = (f32[2,512]{1,0:T(2,128)S(1)}, f32[2,512]{1,0:T(2,128)}, u32[]{:S(2)}) copy-start(f32[2,512]{1,0:T(2,128)} %param.26) | copy-start | bytes 12292
  13.7 8.4 %copy-start.30 = (f32[2,512]{1,0:T(2,128)S(1)}, f32[2,512]{1,0:T(2,128)}, u32[]{:S(2)}) copy-start(f32[2,512]{1,0:T(2,128)} %param.28) | copy-start | bytes 12292
  13.7 9.0 %copy-start.31 = (f32[2,512]{1,0:T(2,128)S(1)}, f32[2,512]{1,0:T(2,128)}, u32[]{:S(2)}) copy-start(f32[2,512]{1,0:T(2,128)} %param.30) | copy-start | bytes 12292
  13.7 9.6 %copy-start.32 = (f32[2,512]{1,0:T(2,128)S(1)}, f32[2,512]{1,0:T(2,128)}, u32[]{:S(2)}) copy-start(f32[2,512]{1,0:T(2,128)} %param.31) | copy-start | bytes 12292
  20.2 15.9 %copy-start.36 = (s32[2560]{0:T(1024)S(1)}, s32[2560]{0:T(1024)}, u32[]{:S(2)}) copy-start(s32[2560]{0:T(1024)} %param.19) | copy-start | bytes 30724
  26.7 17.8 %all-to-all-start.1 = ((bf16[32,8,512]{2,1,0:T(8,128)(2,1)}), bf16[32,8,512]{2,1,0:T(8,128)(2,1)S(1)}, u32[]{:S(2)}, u32[]{:S(2)}) async-start(bf16[32,8,512]{2,1,0:T(8,128)(2,1)} %bitcast.8), calls=%async_computation.1 | async-start | bytes 524288 | tf_op jit(solution)/shard_map/all_to_all | solution.py:31
  52.4 5.0 %copy-start.34 = (f32[1,512]{1,0:T(1,128)S(1)}, f32[1,512]{1,0:T(1,128)}, u32[]{:S(2)}) copy-start(f32[1,512]{1,0:T(1,128)} %get-tuple-element.19) | copy-start | bytes 6148
  72.5 6.3 %copy-start.10 = (f32[320,512]{1,0:T(8,128)S(1)}, f32[320,512]{1,0:T(8,128)}, u32[]{:S(2)}) copy-start(f32[320,512]{1,0:T(8,128)} %convolution_add_fusion.3) | copy-start | bytes 1966084
  72.5 6.3 %copy-start.37 = (s32[2560]{0:T(1024)S(1)}, s32[2560]{0:T(1024)}, u32[]{:S(2)}) copy-start(s32[2560]{0:T(1024)} %param.19) | copy-start | bytes 30724
  78.8 5.4 %copy-start.3 = (f32[2,40,8,256]{3,2,0,1:T(8,128)S(1)}, f32[2,40,8,256]{3,2,0,1:T(8,128)}, u32[]{:S(2)}) copy-start(f32[2,40,8,256]{3,2,0,1:T(8,128)} %copy-done.2) | copy-start | bytes 1966084
  78.8 5.4 %copy-start.17 = (f32[1,512]{1,0:T(1,128)S(1)}, f32[1,512]{1,0:T(1,128)}, u32[]{:S(2)}) copy-start(f32[1,512]{1,0:T(1,128)} %get-tuple-element.11) | copy-start | bytes 6148
  78.8 5.4 %copy-start.19 = (f32[1,512]{1,0:T(1,128)S(1)}, f32[1,512]{1,0:T(1,128)}, u32[]{:S(2)}) copy-start(f32[1,512]{1,0:T(1,128)} %get-tuple-element.13) | copy-start | bytes 6148
  83.4 6.0 %copy-start.11 = (f32[320]{0:T(512)}, f32[320]{0:T(512)S(1)}, u32[]{:S(2)}) copy-start(f32[320]{0:T(512)S(1)} %broadcast_multiply_fusion.3) | copy-start | bytes 3844
  83.7 5.7 %copy-start.15 = (f32[320]{0:T(512)}, f32[320]{0:T(512)S(1)}, u32[]{:S(2)}) copy-start(f32[320]{0:T(512)S(1)} %add_rsqrt_fusion.3) | copy-start | bytes 3844
  86.3 5.9 %copy-start.23 = (f32[1,512]{1,0:T(1,128)S(1)}, f32[1,512]{1,0:T(1,128)}, u32[]{:S(2)}) copy-start(f32[1,512]{1,0:T(1,128)} %get-tuple-element.20) | copy-start | bytes 6148
  89.4 13.3 %all-to-all-start.2 = ((bf16[32,8,512]{2,1,0:T(8,128)(2,1)}), bf16[32,8,512]{2,1,0:T(8,128)(2,1)S(1)}, u32[]{:S(2)}, u32[]{:S(2)}) async-start(bf16[32,8,512]{2,1,0:T(8,128)(2,1)} %bitcast.23), calls=%async_computation.2 | async-start | bytes 524288 | tf_op jit(solution)/shard_map/all_to_all | solution.py:31
  110.4 4.9 %copy-start.33 = (f32[1,512]{1,0:T(1,128)S(1)}, f32[1,512]{1,0:T(1,128)}, u32[]{:S(2)}) copy-start(f32[1,512]{1,0:T(1,128)} %get-tuple-element.18) | copy-start | bytes 6148
  136.6 6.0 %copy-start.9 = (f32[320,512]{1,0:T(8,128)S(1)}, f32[320,512]{1,0:T(8,128)}, u32[]{:S(2)}) copy-start(f32[320,512]{1,0:T(8,128)} %convolution_add_fusion.1) | copy-start | bytes 1966084
  136.6 6.0 %copy-start.38 = (s32[2560]{0:T(1024)S(1)}, s32[2560]{0:T(1024)}, u32[]{:S(2)}) copy-start(s32[2560]{0:T(1024)} %param.19) | copy-start | bytes 30724
  142.6 4.9 %copy-start.4 = (f32[2,40,8,256]{3,2,0,1:T(8,128)S(1)}, f32[2,40,8,256]{3,2,0,1:T(8,128)}, u32[]{:S(2)}) copy-start(f32[2,40,8,256]{3,2,0,1:T(8,128)} %copy-done.2) | copy-start | bytes 1966084
  142.6 4.9 %copy-start.6 = (f32[320,512]{1,0:T(8,128)S(1)}, f32[320,512]{1,0:T(8,128)}, u32[]{:S(2)}) copy-start(f32[320,512]{1,0:T(8,128)} %copy-done.5) | copy-start | bytes 1966084
  (18 other events, 71.9 us)
where the time goes:
time: 150 us; the launch traced here: 149 us
  matrix products  64.7 us (43%)
  local copies, waits for them, and re-layouts  38.7 us (26%)
  other arithmetic  23 us (15%)
  starting transfers between devices  14.2 us (9%)
  waiting for transfers between devices  7.02 us (5%)
    dot_general x8, matrix products, perceptron(): jnp.dot(pieces[position], first_weight[position * columns:(position + 1)...  35.5 us
    dot_general x4, matrix products, perceptron(): result = jnp.dot(active, second_weight, preferred_element_type=jnp.float32)  23 us
    gather x2, local copies, waits for them, and re-layouts, shards(): sender_table[edge_sender]  15.5 us
    unnamed x80, local copies, waits for them, and re-layouts  14.9 us
    add x2, other arithmetic, shards(): edge_state + jnp.where(usable[:, None], update, jnp.zeros_like(update))  12.5 us
    all_to_all x2, starting transfers between devices, fetch_halo(): lax.all_to_all(outgoing, ('patch', 'band'), split_axis=0, concat_axis=0,...  9.93 us
    all_to_all x2, waiting for transfers between devices, fetch_halo(): lax.all_to_all(outgoing, ('patch', 'band'), split_axis=0, concat_axis=0,...  7.02 us
    reduce_sum x4, other arithmetic, layer_norm(): spread = jnp.mean(centre * centre, axis=-1, keepdims=True)  6.93 us
  transfers between devices with their start and end apart: 3, of which 2 were waited for; matrix products, arithmetic and copies ran while one was open for 22% of the time, Pallas kernels for 0%

commit v1 on v0

v1 whole, which is shorter than its diff:
```python
import functools

import jax
import jax.numpy as jnp
from jax import lax
from jax.experimental import pallas as pl
from jax.experimental.pallas import tpu as pltpu
from jax.sharding import PartitionSpec as P

epsilon = 1e-05
f32 = jnp.float32
bf16 = jnp.bfloat16
AXES = ("patch", "band")


def layer_norm(values, norm_gain, norm_offset):
    centre = values - jnp.mean(values, axis=-1, keepdims=True)
    spread = jnp.mean(centre * centre, axis=-1, keepdims=True)
    return centre * lax.rsqrt(spread + epsilon) * norm_gain + norm_offset


def swish(values):
    half = 0.5 * values
    return half * jnp.tanh(half) + half


def matmul(left, right):
    return jnp.dot(left, right, preferred_element_type=f32)


def column(row):
    return jnp.broadcast_to(row, (128, row.shape[1])).T[:, :1]


def one_hot(hits):
    return jnp.where(hits, 1.0, 0.0).astype(bf16)


def lanes(rows, columns):
    return lax.broadcasted_iota(jnp.int32, (rows, columns), 1)


def select_rows(send_ref, node_low):
    hits = column(send_ref[...]) == lanes(send_ref.shape[1], node_low.shape[0])
    return matmul(one_hot(hits), node_low).astype(bf16)


def start_kernel(band_ref, received_ref, latents_ref, send_ref, node_ref, outgoing_ref):
    bands, nodes, width = received_ref.shape
    band = band_ref[0]
    own = latents_ref[pl.ds(pl.multiple_of(band * nodes, 8), nodes), :]
    parts = [
        jnp.where(band == j, own, received_ref[j].astype(f32)) for j in range(bands)
    ]
    node_state = jnp.concatenate(parts, axis=1)
    node_ref[...] = node_state
    outgoing_ref[...] = select_rows(send_ref, node_state.astype(bf16))


def before_kernel(
    node_ref, edge_ref, sender_ref, receiver_ref, weight_ref, bias_ref, pre_ref, table_ref
):
    nodes, width = node_ref.shape

    @pl.when(pl.program_id(0) == 0)
    def _():
        node_low = node_ref[...].astype(bf16)
        for j in (0, 1):
            part = weight_ref[0, (1 + j) * width : (2 + j) * width, :]
            table_ref[j * nodes : (j + 1) * nodes, :] = matmul(node_low, part).astype(bf16)

    sender = sender_ref[0]
    rows = sender.shape[1]
    index = lanes(rows, 2 * nodes)
    local = column(jnp.where(sender < nodes, sender, -1))
    hits = (index == local) | (index == column(receiver_ref[0] + nodes))
    running = matmul(edge_ref[...].astype(bf16), weight_ref[0, :width, :])
    running = running + matmul(one_hot(hits), table_ref[...])
    pre_ref[...] = (running + bias_ref[0]).astype(bf16)


def after_kernel(
    count_ref,
    node_ref,
    incoming_ref,
    pre_ref,
    edge_ref,
    sender_ref,
    receiver_ref,
    first_ref,
    second_ref,
    gain_ref,
    offset_ref,
    node_bias_ref,
    node_gain_ref,
    node_offset_ref,
    send_ref,
    node_first_hbm,
    node_second_hbm,
    new_node_ref,
    new_edge_ref,
    outgoing_ref,
    table_ref,
    sum_ref,
    node_first_ref,
    node_second_ref,
    sems,
    *,
    layer,
    block_length,
):
    nodes, width = node_ref.shape
    step = pl.program_id(0)
    copies = (
        pltpu.make_async_copy(node_first_hbm.at[layer], node_first_ref, sems.at[0]),
        pltpu.make_async_copy(node_second_hbm.at[layer], node_second_ref, sems.at[1]),
    )

    @pl.when(step == 0)
    def _():
        for copy in copies:
            copy.start()
        table_ref[...] = matmul(incoming_ref[...], first_ref[0]).astype(bf16)
        sum_ref[...] = jnp.zeros_like(sum_ref)

    sender = sender_ref[0]
    rows = sender.shape[1]
    blocks = rows // block_length
    hits = column(sender - nodes) == lanes(rows, table_ref.shape[0])
    running = pre_ref[...].astype(f32) + matmul(one_hot(hits), table_ref[...])
    active = swish(running).astype(bf16)
    update = layer_norm(matmul(active, second_ref[0]), gain_ref[0], offset_ref[0])
    spot = lax.broadcasted_iota(jnp.int32, (block_length, 1), 0)
    place = lanes(1, block_length)
    receivers = []
    lows = []
    for j in range(blocks):
        part = slice(j * block_length, (j + 1) * block_length)
        count = count_ref[step * blocks + j]
        state = edge_ref[part, :] + jnp.where(spot < count, update[part], 0.0)
        new_edge_ref[part, :] = state
        lows.append(state.astype(bf16))
        receivers.append(jnp.where(place < count, receiver_ref[0, :, part], -1))
    receiver = jnp.concatenate(receivers, axis=1)
    low = jnp.concatenate(lows, axis=0)
    summing = one_hot(lax.broadcasted_iota(jnp.int32, (nodes, rows), 0) == receiver)
    sum_ref[...] += matmul(summing, low)

    @pl.when(step == pl.num_programs(0) - 1)
    def _():
        for copy in copies:
            copy.wait()
        node_state = node_ref[...]
        running = matmul(node_state.astype(bf16), node_first_ref[:width, :])
        running = running + matmul(sum_ref[...].astype(bf16), node_first_ref[width:, :])
        active = swish(running + node_bias_ref[0]).astype(bf16)
        result = matmul(active, node_second_ref[...])
        node_state = node_state + layer_norm(result, node_gain_ref[0], node_offset_ref[0])
        new_node_ref[...] = node_state
        outgoing_ref[...] = select_rows(send_ref, node_state.astype(bf16))


def whole(shape):
    return pl.BlockSpec(shape, lambda *_: (0,) * len(shape))


def of_layer(shape, layer, row=0):
    return pl.BlockSpec((1,) + shape, lambda *_: (layer, row, 0))


def shards(
    latents,
    edge_latents,
    edge_sender,
    edge_receiver,
    block_counts,
    send_rows,
    edge_first_weight,
    edge_first_bias,
    edge_second_weight,
    edge_gain,
    edge_offset,
    node_first_weight,
    node_first_bias,
    node_second_weight,
    node_gain,
    node_offset,
):
    layers = edge_first_weight.shape[0]
    edges, width = edge_latents.shape
    hidden = edge_first_weight.shape[2]
    bands = width // latents.shape[1]
    nodes = latents.shape[0] // bands
    halo = send_rows.shape[1] * send_rows.shape[2]
    block_length = edges // block_counts.shape[0]
    blocks = max(b for b in range(1, 5) if block_counts.shape[0] % b == 0)
    rows = blocks * block_length
    steps = edges // rows
    senders = edge_sender.reshape(steps, 1, rows)
    receivers = edge_receiver.reshape(steps, 1, rows)
    send_row = send_rows.reshape(1, halo)
    band = lax.axis_index("band").astype(jnp.int32).reshape(1)
    vectors = [
        v.reshape(layers, 1, -1)
        for v in (edge_first_bias, edge_gain, edge_offset, node_first_bias, node_gain, node_offset)
    ]
    first_bias, gain, offset, node_bias, n_gain, n_offset = vectors

    received = lax.all_to_all(
        latents.astype(bf16).reshape(bands, nodes, -1),
        "band", split_axis=0, concat_axis=0, tiled=True,
    )
    node_state, outgoing = pl.pallas_call(
        start_kernel,
        out_shape=(
            jax.ShapeDtypeStruct((nodes, width), f32),
            jax.ShapeDtypeStruct((halo, width), bf16),
        ),
        in_specs=[
            pl.BlockSpec(memory_space=pltpu.SMEM),
            whole(received.shape),
            whole(latents.shape),
            whole(send_row.shape),
        ],
        out_specs=(whole((nodes, width)), whole((halo, width))),
        grid=(1,),
        name="start",
    )(band, received, latents, send_row)

    edge_state = edge_latents
    row_block = pl.BlockSpec((rows, width), lambda s, *_: (s, 0))
    index_block = pl.BlockSpec((1, 1, rows), lambda s, *_: (s, 0, 0))
    for layer in range(layers):
        incoming = lax.all_to_all(
            outgoing.reshape(send_rows.shape[1], send_rows.shape[2], width),
            AXES, split_axis=0, concat_axis=0, tiled=True,
        ).reshape(halo, width)
        pre = pl.pallas_call(
            before_kernel,
            out_shape=jax.ShapeDtypeStruct((edges, hidden), bf16),
            grid=(steps,),
            in_specs=[
                whole((nodes, width)),
                row_block,
                index_block,
                index_block,
                of_layer((3 * width, hidden), layer),
                of_layer((1, hidden), layer),
            ],
            out_specs=pl.BlockSpec((rows, hidden), lambda s, *_: (s, 0)),
            scratch_shapes=[pltpu.VMEM((2 * nodes, hidden), bf16)],
            cost_estimate=pl.CostEstimate(
                flops=2 * edges * hidden * (width + 2 * nodes),
                bytes_accessed=edges * width * 6,
                transcendentals=0,
            ),
            name="before",
        )(node_state, edge_state, senders, receivers, edge_first_weight, first_bias)
        node_state, edge_state, outgoing = pl.pallas_call(
            functools.partial(after_kernel, layer=layer, block_length=block_length),
            out_shape=(
                jax.ShapeDtypeStruct((nodes, width), f32),
                jax.ShapeDtypeStruct((edges, width), f32),
                jax.ShapeDtypeStruct((halo, width), bf16),
            ),
            grid_spec=pltpu.PrefetchScalarGridSpec(
                num_scalar_prefetch=1,
                grid=(steps,),
                in_specs=[
                    whole((nodes, width)),
                    whole((halo, width)),
                    pl.BlockSpec((rows, hidden), lambda s, *_: (s, 0)),
                    row_block,
                    index_block,
                    index_block,
                    of_layer((width, hidden), layer, 1),
                    of_layer((hidden, width), layer),
                    of_layer((1, width), layer),
                    of_layer((1, width), layer),
                    of_layer((1, hidden), layer),
                    of_layer((1, width), layer),
                    of_layer((1, width), layer),
                    whole(send_row.shape),
                    pl.BlockSpec(memory_space=pl.ANY),
                    pl.BlockSpec(memory_space=pl.ANY),
                ],
                out_specs=(
                    whole((nodes, width)),
                    row_block,
                    whole((halo, width)),
                ),
                scratch_shapes=[
                    pltpu.VMEM((halo, hidden), bf16),
                    pltpu.VMEM((nodes, width), f32),
                    pltpu.VMEM(node_first_weight.shape[1:], bf16),
                    pltpu.VMEM(node_second_weight.shape[1:], bf16),
                    pltpu.SemaphoreType.DMA((2,)),
                ],
            ),
            name="after",
        )(
            block_counts,
            node_state,
            incoming,
            pre,
            edge_state,
            senders,
            receivers,
            edge_first_weight,
            edge_second_weight,
            gain,
            offset,
            node_bias,
            n_gain,
            n_offset,
            send_row,
            node_first_weight,
            node_second_weight,
        )
    return (node_state, edge_state)


def solution(mesh):
    split = P(AXES)
    return jax.shard_map(
        shards,
        mesh=mesh,
        in_specs=(
            P("patch", "band"),
            P(AXES, None),
            split,
            split,
            split,
            P(AXES, None, None),
        )
        + (P(),) * 10,
        out_specs=(P(AXES, None), P(AXES, None)),
        check_vma=False,
    )
```

time: 150 us -> 82.9 us (0.55)
  matrix products: 64.7 us -> 0 us
  Pallas kernels: 0 us -> 49.2 us
  local copies, waits for them, and re-layouts: 38.7 us -> 8.39 us
  other arithmetic: 23 us -> 1.89 us
    dot_general x14 -> x0, matrix products: 64.7 us -> none  [the longest x8 35.5 us: perceptron(): jnp.dot(pieces[position], first_weight[position * columns:(position + 1)...]
    pallas_call x0 -> x5, Pallas kernels: none -> 49.2 us  [the longest x2 28.4 us: shards(): pl.pallas_call(functools.partial(after_kernel, layer=layer, block_length=...]
    gather x4 -> x0, local copies, waits for them, and re-layouts: 19.2 us -> none  [the longest x2 15.5 us: shards(): sender_table[edge_sender]]
    add x3 -> x0, other arithmetic: 13.6 us -> none  [the longest x2 12.5 us: shards(): edge_state + jnp.where(usable[:, None], update, jnp.zeros_like(update))]
    unnamed x80 -> x23, local copies, waits for them, and re-layouts: 14.9 us -> 2.97 us
    reduce_sum x4 -> x0, other arithmetic: 6.93 us -> none  [layer_norm(): spread = jnp.mean(centre * centre, axis=-1, keepdims=True)]
    reshape x0 -> x9, local copies, waits for them, and re-layouts: none -> 5.42 us  [the longest x6 3.53 us: shards(): v.reshape(layers, 1, -1)]
    slice x6 -> x0, local copies, waits for them, and re-layouts: 4.34 us -> none  [the longest x1 1.36 us: shards(): edge_first_bias[layer_index]]
  transfers between devices with their start and end apart: 3 -> 3, of which waited for: 2 -> 2; matrix products, arithmetic and copies ran while one was open for 22% -> 8% of each run, Pallas kernels for 0% -> 23%
where the time goes in v1:
time: 82.9 us; the launch traced here: 82 us
  Pallas kernels  49.2 us (59%)
  starting transfers between devices  15.2 us (18%)
  local copies, waits for them, and re-layouts  8.39 us (10%)
  waiting for transfers between devices  6.53 us (8%)
  other arithmetic  1.89 us (2%)
    pallas_call x2, Pallas kernels, shards(): pl.pallas_call(functools.partial(after_kernel, layer=layer, block_length=...  28.4 us
    pallas_call x2, Pallas kernels, shards(): pl.pallas_call(before_kernel, out_shape=jax.ShapeDtypeStruct((edges, hidd...  18.5 us
    all_to_all x2, starting transfers between devices, shards(): lax.all_to_all(outgoing.reshape(send_rows.shape[1], send_rows.shape[2], w...  11 us
    all_to_all x1, waiting for transfers between devices, shards(): lax.all_to_all(latents.astype(bf16).reshape(bands, nodes, -1), 'band', sp...  5.15 us
    all_to_all x1, starting transfers between devices, shards(): lax.all_to_all(latents.astype(bf16).reshape(bands, nodes, -1), 'band', sp...  4.23 us
    reshape x6, local copies, waits for them, and re-layouts, shards(): v.reshape(layers, 1, -1)  3.53 us
    unnamed x23, local copies, waits for them, and re-layouts  2.97 us
    pallas_call x1, Pallas kernels, shards(): pl.pallas_call(start_kernel, out_shape=(jax.ShapeDtypeStruct((nodes, widt...  2.35 us
  transfers between devices with their start and end apart: 3, of which 2 were waited for; matrix products, arithmetic and copies ran while one was open for 8% of the time, Pallas kernels for 23%

profile of v1, /device:TPU:0, one launch (start us, length us, event | category | flops | bytes accessed | tf_op | source)
XLA Modules:
  0.0 82.0 jit_solution(7038922928174956272)
XLA Ops:
  0.7 1.9 %convert_element_type.3 = bf16[640,256]{1,0:T(8,128)(2,1)} convert(f32[640,256]{1,0:T(8,128)} %latents_ref.1) | non-fusion elementwise | flops 163840 | bytes 983040 | tf_op jit(solution)/shard_map/convert_element_type | solution.py:210
  2.6 4.2 %all-to-all-start = ((bf16[2,320,256]{2,1,0:T(8,128)(2,1)}), bf16[2,320,256]{2,1,0:T(8,128)(2,1)S(1)}, u32[]{:S(2)}, u32[]{:S(2)}) async-start(bf16[2,320,256]{2,1,0:T(8,128)(2,1)} %bitcast.1), calls=%async_computation | async-start | bytes 655360 | tf_op jit(solution)/shard_map/all_to_all | solution.py:209
  6.8 0.8 copy.19
  7.6 0.7 reshape.51.send_ref
  8.3 5.2 %all-to-all-done.received_ref = bf16[2,320,256]{2,1,0:T(8,128)(2,1)S(1)} async-done(((bf16[2,320,256]{2,1,0:T(8,128)(2,1)}), bf16[2,320,256]{2,1,0:T(8,128)(2,1)S(1)}, u32[]{:S(2)}, u32[]{:S(2)}) %all-to-all-start) | async-done | bytes 327712 | tf_op jit(solution)/shard_map/all_to_all | solution.py:209
  13.4 0.7 copy-done
  14.1 2.4 %start.1 = (f32[320,512]{1,0:T(8,128)}, bf16[256,512]{1,0:T(8,128)(2,1)}) custom-call(s32[1]{0:T(128)} %bitcast.band_ref, bf16[2,320,256]{2,1,0:T(8,128)(2,1)} %copy-done, f32[640,256]{1,0:T(8,128)} %latents_ref.1, s32[1,256]{1,0:T(1,128)} %reshape.51.send_ref), custom_call_target="tpu_custom_call" | custom-call | tf_op jit(solution)/shard_map/start/pallas_call | solution.py:213
  16.5 5.2 %all-to-all-start.1 = ((bf16[32,8,512]{2,1,0:T(8,128)(2,1)}), bf16[32,8,512]{2,1,0:T(8,128)(2,1)S(1)}, u32[]{:S(2)}, u32[]{:S(2)}) async-start(bf16[32,8,512]{2,1,0:T(8,128)(2,1)} %bitcast.8), calls=%async_computation.1 | async-start | bytes 524288 | tf_op jit(solution)/shard_map/all_to_all | solution.py:234
  21.7 0.6 reshape.56.bias_ref
  22.3 0.6 reshape.57.gain_ref
  22.9 0.6 reshape.58.offset_ref
  23.5 0.6 reshape.59.node_bias_ref
  24.1 0.6 reshape.60.node_gain_ref
  24.6 0.6 reshape.61.node_offset_ref
  25.2 0.6 reshape.54.sender_ref
  25.9 0.6 reshape.55.receiver_ref
  26.5 9.3 %before.2.pre_ref = bf16[2560,512]{1,0:T(8,128)(2,1)} custom-call(f32[320,512]{1,0:T(8,128)} %get-tuple-element.9.node_ref, f32[2560,512]{1,0:T(8,128)} %edge_ref.3, s32[5,1,512]{2,1,0:T(1,128)} %reshape.54.sender_ref, s32[5,1,512]{2,1,0:T(1,128)} %reshape.55.receiver_ref, bf16[2,1536,512]{2,1,0:T(8,128)(2,1)} %first_ref.3, f32[2,1,512]{2,1,0:T(1,128)} %reshape.56.bias_ref), custom_call_target="tpu_custom_call" | custom-call | flops 3019898880 | bytes 7864320 | tf_op jit(solution)/shard_map/before/pallas_call | solution.py:238
  35.7 0.7 copy-done.2
  36.4 14.2 %after.2 = (f32[320,512]{1,0:T(8,128)}, f32[2560,512]{1,0:T(8,128)}, bf16[256,512]{1,0:T(8,128)(2,1)}) custom-call(s32[20]{0:T(128)} %count_ref.3, f32[320,512]{1,0:T(8,128)} %get-tuple-element.9.node_ref, bf16[256,512]{1,0:T(8,128)(2,1)} %bitcast.7, bf16[2560,512]{1,0:T(8,128)(2,1)} %before.2.pre_ref, f32[2560,512]{1,0:T(8,128)} %edge_ref.3, ...), custom_call_target="tpu_custom_call" | custom-call | tf_op jit(solution)/shard_map/after/pallas_call | solution.py:259
  50.7 5.8 %all-to-all-start.2 = ((bf16[32,8,512]{2,1,0:T(8,128)(2,1)}), bf16[32,8,512]{2,1,0:T(8,128)(2,1)S(1)}, u32[]{:S(2)}, u32[]{:S(2)}) async-start(bf16[32,8,512]{2,1,0:T(8,128)(2,1)} %bitcast.9), calls=%async_computation.2 | async-start | bytes 524288 | tf_op jit(solution)/shard_map/all_to_all | solution.py:234
  56.5 9.3 %before.3.pre_ref = bf16[2560,512]{1,0:T(8,128)(2,1)} custom-call(f32[320,512]{1,0:T(8,128)} %get-tuple-element.11.node_ref, f32[2560,512]{1,0:T(8,128)} %get-tuple-element.13.edge_ref, s32[5,1,512]{2,1,0:T(1,128)} %reshape.54.sender_ref, s32[5,1,512]{2,1,0:T(1,128)} %reshape.55.receiver_ref, bf16[2,1536,512]{2,1,0:T(8,128)(2,1)} %first_ref.3, ...), custom_call_target="tpu_custom_call" | custom-call | flops 3019898880 | bytes 7864320 | tf_op jit(solution)/shard_map/before/pallas_call | solution.py:238
  65.8 1.4 %all-to-all-done.2 = bf16[32,8,512]{2,1,0:T(8,128)(2,1)S(1)} async-done(((bf16[32,8,512]{2,1,0:T(8,128)(2,1)}), bf16[32,8,512]{2,1,0:T(8,128)(2,1)S(1)}, u32[]{:S(2)}, u32[]{:S(2)}) %all-to-all-start.2) | async-done | bytes 262176 | tf_op jit(solution)/shard_map/all_to_all | solution.py:234
  67.2 0.7 copy-done.1
  67.9 14.1 %after.3 = (f32[320,512]{1,0:T(8,128)}, f32[2560,512]{1,0:T(8,128)}, bf16[256,512]{1,0:T(8,128)(2,1)}) custom-call(s32[20]{0:T(128)} %count_ref.3, f32[320,512]{1,0:T(8,128)} %get-tuple-element.11.node_ref, bf16[256,512]{1,0:T(8,128)(2,1)} %bitcast.6, bf16[2560,512]{1,0:T(8,128)(2,1)} %before.3.pre_ref, f32[2560,512]{1,0:T(8,128)} %get-tuple-element.13.edge_ref, ...), custom_call_target="tpu_custom_call" | custom-call | tf_op jit(solution)/shard_map/after/pallas_call | solution.py:259
  (20 shorter events, 0.0 us)
Async XLA Ops:
  0.6 21.1 %copy-start.5 = (f32[2,512]{1,0:T(2,128)S(1)}, f32[2,512]{1,0:T(2,128)}, u32[]{:S(2)}) copy-start(f32[2,512]{1,0:T(2,128)} %param.23) | copy-start | bytes 12292
  0.6 21.6 %copy-start.6 = (f32[2,512]{1,0:T(2,128)S(1)}, f32[2,512]{1,0:T(2,128)}, u32[]{:S(2)}) copy-start(f32[2,512]{1,0:T(2,128)} %param.25) | copy-start | bytes 12292
  0.7 22.2 %copy-start.7 = (f32[2,512]{1,0:T(2,128)S(1)}, f32[2,512]{1,0:T(2,128)}, u32[]{:S(2)}) copy-start(f32[2,512]{1,0:T(2,128)} %param.26) | copy-start | bytes 12292
  0.7 22.8 %copy-start.8 = (f32[2,512]{1,0:T(2,128)S(1)}, f32[2,512]{1,0:T(2,128)}, u32[]{:S(2)}) copy-start(f32[2,512]{1,0:T(2,128)} %param.28) | copy-start | bytes 12292
  0.7 23.4 %copy-start.9 = (f32[2,512]{1,0:T(2,128)S(1)}, f32[2,512]{1,0:T(2,128)}, u32[]{:S(2)}) copy-start(f32[2,512]{1,0:T(2,128)} %param.30) | copy-start | bytes 12292
  0.7 24.0 %copy-start.10 = (f32[2,512]{1,0:T(2,128)S(1)}, f32[2,512]{1,0:T(2,128)}, u32[]{:S(2)}) copy-start(f32[2,512]{1,0:T(2,128)} %param.31) | copy-start | bytes 12292
  0.7 24.6 %copy-start.3 = (s32[2560]{0:T(1024)S(1)}, s32[2560]{0:T(1024)}, u32[]{:S(2)}) copy-start(s32[2560]{0:T(1024)} %param.18) | copy-start | bytes 30724
  0.7 25.2 %copy-start.4 = (s32[2560]{0:T(1024)S(1)}, s32[2560]{0:T(1024)}, u32[]{:S(2)}) copy-start(s32[2560]{0:T(1024)} %param.19) | copy-start | bytes 30724
  2.6 10.8 %all-to-all-start = ((bf16[2,320,256]{2,1,0:T(8,128)(2,1)}), bf16[2,320,256]{2,1,0:T(8,128)(2,1)S(1)}, u32[]{:S(2)}, u32[]{:S(2)}) async-start(bf16[2,320,256]{2,1,0:T(8,128)(2,1)} %bitcast.1), calls=%async_computation | async-start | bytes 655360 | tf_op jit(solution)/shard_map/all_to_all | solution.py:209
  13.4 0.7 copy-start
  16.5 19.2 %all-to-all-start.1 = ((bf16[32,8,512]{2,1,0:T(8,128)(2,1)}), bf16[32,8,512]{2,1,0:T(8,128)(2,1)S(1)}, u32[]{:S(2)}, u32[]{:S(2)}) async-start(bf16[32,8,512]{2,1,0:T(8,128)(2,1)} %bitcast.8), calls=%async_computation.1 | async-start | bytes 524288 | tf_op jit(solution)/shard_map/all_to_all | solution.py:234
  35.7 0.7 copy-start.2
  50.7 16.5 %all-to-all-start.2 = ((bf16[32,8,512]{2,1,0:T(8,128)(2,1)}), bf16[32,8,512]{2,1,0:T(8,128)(2,1)S(1)}, u32[]{:S(2)}, u32[]{:S(2)}) async-start(bf16[32,8,512]{2,1,0:T(8,128)(2,1)} %bitcast.9), calls=%async_computation.2 | async-start | bytes 524288 | tf_op jit(solution)/shard_map/all_to_all | solution.py:234
  67.2 0.7 copy-start.1

commit v2 on v1

--- a/solution.py
+++ b/solution.py
@@ -11,6 +11,9 @@
 f32 = jnp.float32
 bf16 = jnp.bfloat16
 AXES = ("patch", "band")
+STEP = 5
+CHUNK = 5
+LIMIT = 32 * 1024 * 1024
 
 
 def layer_norm(values, norm_gain, norm_offset):
@@ -58,7 +61,7 @@
 
 
 def before_kernel(
-    node_ref, edge_ref, sender_ref, receiver_ref, weight_ref, bias_ref, pre_ref, table_ref
+    node_ref, edge_ref, sender_ref, receiver_ref, weight_ref, bias_ref, pre_ref, table_ref, *, layer, chunk
 ):
     nodes, width = node_ref.shape
 
@@ -69,14 +72,19 @@
             part = weight_ref[0, (1 + j) * width : (2 + j) * width, :]
             table_ref[j * nodes : (j + 1) * nodes, :] = matmul(node_low, part).astype(bf16)
 
-    sender = sender_ref[0]
-    rows = sender.shape[1]
-    index = lanes(rows, 2 * nodes)
-    local = column(jnp.where(sender < nodes, sender, -1))
-    hits = (index == local) | (index == column(receiver_ref[0] + nodes))
-    running = matmul(edge_ref[...].astype(bf16), weight_ref[0, :width, :])
-    running = running + matmul(one_hot(hits), table_ref[...])
-    pre_ref[...] = (running + bias_ref[0]).astype(bf16)
+    index = lanes(chunk, 2 * nodes)
+    rows = sender_ref.shape[2]
+    base = pl.multiple_of(pl.program_id(0) * rows, rows)
+    for start in range(0, rows, chunk):
+        part = slice(start, start + chunk)
+        at = pl.ds(base + start, chunk)
+        edge = edge_ref[part, :]
+        sender = sender_ref[0, :, part]
+        local = column(jnp.where(sender < nodes, sender, -1))
+        hits = (index == local) | (index == column(receiver_ref[0, :, part] + nodes))
+        running = matmul(edge.astype(bf16), weight_ref[0, :width, :])
+        running = running + matmul(one_hot(hits), table_ref[...])
+        pre_ref[at, :] = (running + bias_ref[layer : layer + 1, :]).astype(bf16)
 
 
 def after_kernel(
@@ -108,6 +116,7 @@
     *,
     layer,
     block_length,
+    chunk,
 ):
     nodes, width = node_ref.shape
     step = pl.program_id(0)
@@ -123,28 +132,33 @@
         table_ref[...] = matmul(incoming_ref[...], first_ref[0]).astype(bf16)
         sum_ref[...] = jnp.zeros_like(sum_ref)
 
-    sender = sender_ref[0]
-    rows = sender.shape[1]
+    rows = sender_ref.shape[2]
+    base = pl.multiple_of(step * rows, rows)
     blocks = rows // block_length
-    hits = column(sender - nodes) == lanes(rows, table_ref.shape[0])
-    running = pre_ref[...].astype(f32) + matmul(one_hot(hits), table_ref[...])
-    active = swish(running).astype(bf16)
-    update = layer_norm(matmul(active, second_ref[0]), gain_ref[0], offset_ref[0])
     spot = lax.broadcasted_iota(jnp.int32, (block_length, 1), 0)
     place = lanes(1, block_length)
-    receivers = []
-    lows = []
-    for j in range(blocks):
-        part = slice(j * block_length, (j + 1) * block_length)
-        count = count_ref[step * blocks + j]
-        state = edge_ref[part, :] + jnp.where(spot < count, update[part], 0.0)
-        new_edge_ref[part, :] = state
-        lows.append(state.astype(bf16))
-        receivers.append(jnp.where(place < count, receiver_ref[0, :, part], -1))
-    receiver = jnp.concatenate(receivers, axis=1)
-    low = jnp.concatenate(lows, axis=0)
-    summing = one_hot(lax.broadcasted_iota(jnp.int32, (nodes, rows), 0) == receiver)
-    sum_ref[...] += matmul(summing, low)
+    gain = gain_ref[layer : layer + 1, :]
+    offset = offset_ref[layer : layer + 1, :]
+    for start in range(0, rows, chunk):
+        part = slice(start, start + chunk)
+        hits = column(sender_ref[0, :, part] - nodes) == lanes(chunk, table_ref.shape[0])
+        running = pre_ref[pl.ds(base + start, chunk), :].astype(f32) + matmul(one_hot(hits), table_ref[...])
+        active = swish(running).astype(bf16)
+        update = layer_norm(matmul(active, second_ref[0]), gain, offset)
+        receivers = []
+        lows = []
+        for inner in range(0, chunk, block_length):
+            at = slice(start + inner, start + inner + block_length)
+            count = count_ref[step * blocks + (start + inner) // block_length]
+            change = jnp.where(spot < count, update[inner : inner + block_length], 0.0)
+            state = edge_ref[at, :] + change
+            new_edge_ref[at, :] = state
+            lows.append(state.astype(bf16))
+            receivers.append(jnp.where(place < count, receiver_ref[0, :, at], -1))
+        receiver = jnp.concatenate(receivers, axis=1)
+        low = jnp.concatenate(lows, axis=0)
+        summing = one_hot(lax.broadcasted_iota(jnp.int32, (nodes, chunk), 0) == receiver)
+        sum_ref[...] += matmul(summing, low)
 
     @pl.when(step == pl.num_programs(0) - 1)
     def _():
@@ -153,11 +167,19 @@
         node_state = node_ref[...]
         running = matmul(node_state.astype(bf16), node_first_ref[:width, :])
         running = running + matmul(sum_ref[...].astype(bf16), node_first_ref[width:, :])
-        active = swish(running + node_bias_ref[0]).astype(bf16)
+        active = swish(running + node_bias_ref[layer : layer + 1, :]).astype(bf16)
         result = matmul(active, node_second_ref[...])
-        node_state = node_state + layer_norm(result, node_gain_ref[0], node_offset_ref[0])
+        node_state = node_state + layer_norm(result, node_gain_ref[layer : layer + 1, :], node_offset_ref[layer : layer + 1, :])
         new_node_ref[...] = node_state
         outgoing_ref[...] = select_rows(send_ref, node_state.astype(bf16))
+
+
+def in_hbm(*arrays):
+    return tuple(pltpu.with_memory_space_constraint(a, pltpu.HBM) for a in arrays)
+
+
+def largest(total, limit):
+    return max(b for b in range(1, limit + 1) if total % b == 0)
 
 
 def whole(shape):
@@ -186,6 +208,13 @@
     node_gain,
     node_offset,
 ):
+    edge_first_weight, edge_first_bias, edge_second_weight, edge_gain, edge_offset = in_hbm(
+        edge_first_weight, edge_first_bias, edge_second_weight, edge_gain, edge_offset
+    )
+    node_first_weight, node_first_bias, node_second_weight, node_gain, node_offset = in_hbm(
+        node_first_weight, node_first_bias, node_second_weight, node_gain, node_offset
+    )
+    (own_latents,) = in_hbm(latents)
     layers = edge_first_weight.shape[0]
     edges, width = edge_latents.shape
     hidden = edge_first_weight.shape[2]
@@ -193,19 +222,15 @@
     nodes = latents.shape[0] // bands
     halo = send_rows.shape[1] * send_rows.shape[2]
     block_length = edges // block_counts.shape[0]
-    blocks = max(b for b in range(1, 5) if block_counts.shape[0] % b == 0)
+    blocks = largest(block_counts.shape[0], STEP)
     rows = blocks * block_length
+    chunk = largest(rows // block_length, CHUNK) * block_length
     steps = edges // rows
     senders = edge_sender.reshape(steps, 1, rows)
     receivers = edge_receiver.reshape(steps, 1, rows)
     send_row = send_rows.reshape(1, halo)
+    senders, receivers, send_row = in_hbm(senders, receivers, send_row)
     band = lax.axis_index("band").astype(jnp.int32).reshape(1)
-    vectors = [
-        v.reshape(layers, 1, -1)
-        for v in (edge_first_bias, edge_gain, edge_offset, node_first_bias, node_gain, node_offset)
-    ]
-    first_bias, gain, offset, node_bias, n_gain, n_offset = vectors
-
     received = lax.all_to_all(
         latents.astype(bf16).reshape(bands, nodes, -1),
         "band", split_axis=0, concat_axis=0, tiled=True,
@@ -213,8 +238,8 @@
     node_state, outgoing = pl.pallas_call(
         start_kernel,
         out_shape=(
-            jax.ShapeDtypeStruct((nodes, width), f32),
-            jax.ShapeDtypeStruct((halo, width), bf16),
+            pltpu.HBM((nodes, width), f32),
+            pltpu.HBM((halo, width), bf16),
         ),
         in_specs=[
             pl.BlockSpec(memory_space=pltpu.SMEM),
@@ -224,20 +249,24 @@
         ],
         out_specs=(whole((nodes, width)), whole((halo, width))),
         grid=(1,),
+        compiler_params=pltpu.CompilerParams(vmem_limit_bytes=LIMIT),
         name="start",
-    )(band, received, latents, send_row)
+    )(band, received, own_latents, send_row)
 
     edge_state = edge_latents
+    resident = pl.BlockSpec(memory_space=pltpu.VMEM)
     row_block = pl.BlockSpec((rows, width), lambda s, *_: (s, 0))
     index_block = pl.BlockSpec((1, 1, rows), lambda s, *_: (s, 0, 0))
     for layer in range(layers):
         incoming = lax.all_to_all(
-            outgoing.reshape(send_rows.shape[1], send_rows.shape[2], width),
+            jnp.reshape(outgoing, (send_rows.shape[1], send_rows.shape[2], width)),
             AXES, split_axis=0, concat_axis=0, tiled=True,
         ).reshape(halo, width)
+        (node_state,) = in_hbm(node_state)
+        (edge_state,) = in_hbm(edge_state)
         pre = pl.pallas_call(
-            before_kernel,
-            out_shape=jax.ShapeDtypeStruct((edges, hidden), bf16),
+            functools.partial(before_kernel, layer=layer, chunk=chunk),
+            out_shape=pltpu.VMEM((edges, hidden), bf16),
             grid=(steps,),
             in_specs=[
                 whole((nodes, width)),
@@ -245,9 +274,10 @@
                 index_block,
                 index_block,
                 of_layer((3 * width, hidden), layer),
-                of_layer((1, hidden), layer),
+                whole((layers, width)),
             ],
-            out_specs=pl.BlockSpec((rows, hidden), lambda s, *_: (s, 0)),
+            out_specs=resident,
+            compiler_params=pltpu.CompilerParams(vmem_limit_bytes=LIMIT),
             scratch_shapes=[pltpu.VMEM((2 * nodes, hidden), bf16)],
             cost_estimate=pl.CostEstimate(
                 flops=2 * edges * hidden * (width + 2 * nodes),
@@ -255,13 +285,13 @@
                 transcendentals=0,
             ),
             name="before",
-        )(node_state, edge_state, senders, receivers, edge_first_weight, first_bias)
+        )(node_state, edge_state, senders, receivers, edge_first_weight, edge_first_bias)
         node_state, edge_state, outgoing = pl.pallas_call(
-            functools.partial(after_kernel, layer=layer, block_length=block_length),
+            functools.partial(after_kernel, layer=layer, block_length=block_length, chunk=chunk),
             out_shape=(
-                jax.ShapeDtypeStruct((nodes, width), f32),
-                jax.ShapeDtypeStruct((edges, width), f32),
-                jax.ShapeDtypeStruct((halo, width), bf16),
+                pltpu.HBM((nodes, width), f32),
+                pltpu.HBM((edges, width), f32),
+                pltpu.HBM((halo, width), bf16),
             ),
             grid_spec=pltpu.PrefetchScalarGridSpec(
                 num_scalar_prefetch=1,
@@ -269,17 +299,17 @@
                 in_specs=[
                     whole((nodes, width)),
                     whole((halo, width)),
-                    pl.BlockSpec((rows, hidden), lambda s, *_: (s, 0)),
+                    resident,
                     row_block,
                     index_block,
                     index_block,
                     of_layer((width, hidden), layer, 1),
                     of_layer((hidden, width), layer),
-                    of_layer((1, width), layer),
-                    of_layer((1, width), layer),
-                    of_layer((1, hidden), layer),
-                    of_layer((1, width), layer),
-                    of_layer((1, width), layer),
+                    whole((layers, width)),
+                    whole((layers, width)),
+                    whole((layers, width)),
+                    whole((layers, width)),
+                    whole((layers, width)),
                     whole(send_row.shape),
                     pl.BlockSpec(memory_space=pl.ANY),
                     pl.BlockSpec(memory_space=pl.ANY),
@@ -297,6 +327,7 @@
                     pltpu.SemaphoreType.DMA((2,)),
                 ],
             ),
+            compiler_params=pltpu.CompilerParams(vmem_limit_bytes=LIMIT),
             name="after",
         )(
             block_counts,
@@ -308,11 +339,11 @@
             receivers,
             edge_first_weight,
             edge_second_weight,
-            gain,
-            offset,
-            node_bias,
-            n_gain,
-            n_offset,
+            edge_gain,
+            edge_offset,
+            node_first_bias,
+            node_gain,
+            node_offset,
             send_row,
             node_first_weight,
             node_second_weight,

time: 82.9 us -> 72.3 us (0.87)
  Pallas kernels: 49.2 us -> 43.1 us
  local copies, waits for them, and re-layouts: 8.39 us -> 2.65 us
  waiting for transfers between devices: 6.53 us -> 9.89 us
  starting transfers between devices: 15.2 us -> 13.5 us
    reshape x6 -> x0, local copies, waits for them, and re-layouts: 3.53 us -> none  [shards(): v.reshape(layers, 1, -1)]
    all_to_all x2, waiting for transfers between devices: 1.38 us -> 4.73 us  [shards(): lax.all_to_all(jnp.reshape(outgoing, (send_rows.shape[1], send_rows.shape...]
    pallas_call x3, Pallas kernels: 20.9 us -> 17.6 us  [the longest x2 15.4 us: shards(): pl.pallas_call(functools.partial(before_kernel, layer=layer, chunk=chunk)...]
    pallas_call x2, Pallas kernels: 28.4 us -> 25.5 us  [shards(): pl.pallas_call(functools.partial(after_kernel, layer=layer, block_length=...]
    unnamed x23 -> x7, local copies, waits for them, and re-layouts: 2.97 us -> 0.77 us
    all_to_all x2, starting transfers between devices: 11 us -> 9.28 us  [shards(): lax.all_to_all(jnp.reshape(outgoing, (send_rows.shape[1], send_rows.shape...]
  transfers between devices with their start and end apart: 3 -> 3, of which waited for: 2 -> 3; matrix products, arithmetic and copies ran while one was open for 8% -> 4% of each run, Pallas kernels for 23% -> 21%
where the time goes in v2:
time: 72.3 us; the launch traced here: 71.7 us
  Pallas kernels  43.1 us (60%)
  starting transfers between devices  13.5 us (19%)
  waiting for transfers between devices  9.89 us (14%)
  local copies, waits for them, and re-layouts  2.65 us (4%)
  other arithmetic  1.86 us (3%)
    pallas_call x2, Pallas kernels, shards(): pl.pallas_call(functools.partial(after_kernel, layer=layer, block_length=...  25.5 us
    pallas_call x2, Pallas kernels, shards(): pl.pallas_call(functools.partial(before_kernel, layer=layer, chunk=chunk)...  15.4 us
    all_to_all x2, starting transfers between devices, shards(): lax.all_to_all(jnp.reshape(outgoing, (send_rows.shape[1], send_rows.shape...  9.28 us
    all_to_all x1, waiting for transfers between devices, shards(): lax.all_to_all(latents.astype(bf16).reshape(bands, nodes, -1), 'band', sp...  5.16 us
    all_to_all x2, waiting for transfers between devices, shards(): lax.all_to_all(jnp.reshape(outgoing, (send_rows.shape[1], send_rows.shape...  4.73 us
    all_to_all x1, starting transfers between devices, shards(): lax.all_to_all(latents.astype(bf16).reshape(bands, nodes, -1), 'band', sp...  4.23 us
    pallas_call x1, Pallas kernels, shards(): pl.pallas_call(start_kernel, out_shape=(pltpu.HBM((nodes, width), f32), p...  2.28 us
    convert_element_type x1, other arithmetic, shards(): latents.astype(bf16).reshape(bands, nodes, -1)  1.86 us
  transfers between devices with their start and end apart: 3, of which 3 were waited for; matrix products, arithmetic and copies ran while one was open for 4% of the time, Pallas kernels for 21%

profile of v2, /device:TPU:0, one launch (start us, length us, event | category | flops | bytes accessed | tf_op | source)
XLA Modules:
  0.0 71.7 jit_solution(1689440043510604227)
XLA Ops:
  0.6 0.0 copy-start.1
  0.6 0.0 copy-start.2
  0.6 1.9 %convert_element_type.3 = bf16[640,256]{1,0:T(8,128)(2,1)} convert(f32[640,256]{1,0:T(8,128)} %latents_ref.1) | non-fusion elementwise | flops 163840 | bytes 983040 | tf_op jit(solution)/shard_map/convert_element_type | solution.py:235
  2.5 4.2 %all-to-all-start = ((bf16[2,320,256]{2,1,0:T(8,128)(2,1)}), bf16[2,320,256]{2,1,0:T(8,128)(2,1)S(1)}, u32[]{:S(2)}, u32[]{:S(2)}) async-start(bf16[2,320,256]{2,1,0:T(8,128)(2,1)} %bitcast.1), calls=%async_computation | async-start | bytes 655360 | tf_op jit(solution)/shard_map/all_to_all | solution.py:234
  6.7 0.8 %copy.19 = s32[1,32,8]{2,1,0:T(8,128)S(1)} copy(s32[1,32,8]{1,2,0:T(8,128)} %param.21) | data formatting | bytes 2048 | tf_op args[5]
  7.5 0.7 reshape.33.send_ref
  8.2 5.2 %all-to-all-done.received_ref = bf16[2,320,256]{2,1,0:T(8,128)(2,1)S(1)} async-done(((bf16[2,320,256]{2,1,0:T(8,128)(2,1)}), bf16[2,320,256]{2,1,0:T(8,128)(2,1)S(1)}, u32[]{:S(2)}, u32[]{:S(2)}) %all-to-all-start) | async-done | bytes 327712 | tf_op jit(solution)/shard_map/all_to_all | solution.py:234
  13.3 2.3 %start.1 = (f32[320,512]{1,0:T(8,128)}, bf16[256,512]{1,0:T(8,128)(2,1)}) custom-call(s32[1]{0:T(128)} %bitcast.band_ref, bf16[2,320,256]{2,1,0:T(8,128)(2,1)S(1)} %all-to-all-done.received_ref, f32[640,256]{1,0:T(8,128)} %latents_ref.1, s32[1,256]{1,0:T(1,128)} %reshape.33.send_ref), custom_call_target="tpu_custom_call" | custom-call | tf_op jit(solution)/shard_map/start/pallas_call | solution.py:238
  15.6 5.2 %all-to-all-start.1 = ((bf16[32,8,512]{2,1,0:T(8,128)(2,1)}), bf16[32,8,512]{2,1,0:T(8,128)(2,1)S(1)}, u32[]{:S(2)}, u32[]{:S(2)}) async-start(bf16[32,8,512]{2,1,0:T(8,128)(2,1)} %bitcast.8), calls=%async_computation.1 | async-start | bytes 524288 | tf_op jit(solution)/shard_map/all_to_all | solution.py:261
  20.8 0.0 copy-done.1
  20.8 0.6 reshape.36.sender_ref
  21.4 0.0 copy-done.2
  21.4 0.6 reshape.37.receiver_ref
  22.0 0.0 copy-start
  22.0 7.7 %before.2.pre_ref = bf16[2560,512]{1,0:T(8,128)(2,1)S(1)} custom-call(f32[320,512]{1,0:T(8,128)} %get-tuple-element.9.node_ref, f32[2560,512]{1,0:T(8,128)} %edge_ref.3, s32[4,1,640]{2,1,0:T(1,128)} %reshape.36.sender_ref, s32[4,1,640]{2,1,0:T(1,128)} %reshape.37.receiver_ref, bf16[2,1536,512]{2,1,0:T(8,128)(2,1)} %first_ref.3, f32[2,512]{1,0:T(2,128)} %bias_ref.3), custom_call_target="tpu_custom_call" | custom-call | flops 3019898880 | bytes 7864320 | tf_op jit(solution)/shard_map/before/pallas_call | solution.py:267
  29.7 1.8 %all-to-all-done.1 = bf16[32,8,512]{2,1,0:T(8,128)(2,1)S(1)} async-done(((bf16[32,8,512]{2,1,0:T(8,128)(2,1)}), bf16[32,8,512]{2,1,0:T(8,128)(2,1)S(1)}, u32[]{:S(2)}, u32[]{:S(2)}) %all-to-all-start.1) | async-done | bytes 262176 | tf_op jit(solution)/shard_map/all_to_all | solution.py:261
  31.5 0.0 copy-done
  31.5 12.7 %after.2 = (f32[320,512]{1,0:T(8,128)}, f32[2560,512]{1,0:T(8,128)}, bf16[256,512]{1,0:T(8,128)(2,1)}) custom-call(s32[20]{0:T(128)S(1)} %copy-done, f32[320,512]{1,0:T(8,128)} %get-tuple-element.9.node_ref, bf16[256,512]{1,0:T(8,128)(2,1)S(1)} %bitcast.7, bf16[2560,512]{1,0:T(8,128)(2,1)S(1)} %before.2.pre_ref, f32[2560,512]{1,0:T(8,128)} %edge_ref.3, ...), custom_call_target="tpu_custom_call" | custom-call | tf_op jit(solution)/shard_map/after/pallas_call | solution.py:289
  44.2 4.1 %all-to-all-start.2 = ((bf16[32,8,512]{2,1,0:T(8,128)(2,1)}), bf16[32,8,512]{2,1,0:T(8,128)(2,1)S(1)}, u32[]{:S(2)}, u32[]{:S(2)}) async-start(bf16[32,8,512]{2,1,0:T(8,128)(2,1)} %bitcast.9), calls=%async_computation.2 | async-start | bytes 524288 | tf_op jit(solution)/shard_map/all_to_all | solution.py:261
  48.3 7.7 %before.3.pre_ref = bf16[2560,512]{1,0:T(8,128)(2,1)S(1)} custom-call(f32[320,512]{1,0:T(8,128)} %get-tuple-element.11.node_ref, f32[2560,512]{1,0:T(8,128)} %get-tuple-element.13.edge_ref, s32[4,1,640]{2,1,0:T(1,128)} %reshape.36.sender_ref, s32[4,1,640]{2,1,0:T(1,128)} %reshape.37.receiver_ref, bf16[2,1536,512]{2,1,0:T(8,128)(2,1)} %first_ref.3, ...), custom_call_target="tpu_custom_call" | custom-call | flops 3019898880 | bytes 7864320 | tf_op jit(solution)/shard_map/before/pallas_call | solution.py:267
  56.0 3.0 %all-to-all-done.2 = bf16[32,8,512]{2,1,0:T(8,128)(2,1)S(1)} async-done(((bf16[32,8,512]{2,1,0:T(8,128)(2,1)}), bf16[32,8,512]{2,1,0:T(8,128)(2,1)S(1)}, u32[]{:S(2)}, u32[]{:S(2)}) %all-to-all-start.2) | async-done | bytes 262176 | tf_op jit(solution)/shard_map/all_to_all | solution.py:261
  59.0 12.7 %after.3 = (f32[320,512]{1,0:T(8,128)}, f32[2560,512]{1,0:T(8,128)}, bf16[256,512]{1,0:T(8,128)(2,1)}) custom-call(s32[20]{0:T(128)S(1)} %copy-done, f32[320,512]{1,0:T(8,128)} %get-tuple-element.11.node_ref, bf16[256,512]{1,0:T(8,128)(2,1)S(1)} %bitcast.6, bf16[2560,512]{1,0:T(8,128)(2,1)S(1)} %before.3.pre_ref, f32[2560,512]{1,0:T(8,128)} %get-tuple-element.13.edge_ref, ...), custom_call_target="tpu_custom_call" | custom-call | tf_op jit(solution)/shard_map/after/pallas_call | solution.py:289
Async XLA Ops:
  0.6 20.2 %copy-start.1 = (s32[2560]{0:T(1024)S(1)}, s32[2560]{0:T(1024)}, u32[]{:S(2)}) copy-start(s32[2560]{0:T(1024)} %param.18) | copy-start | bytes 30724
  0.6 20.8 %copy-start.2 = (s32[2560]{0:T(1024)S(1)}, s32[2560]{0:T(1024)}, u32[]{:S(2)}) copy-start(s32[2560]{0:T(1024)} %param.19) | copy-start | bytes 30724
  2.5 10.8 %all-to-all-start = ((bf16[2,320,256]{2,1,0:T(8,128)(2,1)}), bf16[2,320,256]{2,1,0:T(8,128)(2,1)S(1)}, u32[]{:S(2)}, u32[]{:S(2)}) async-start(bf16[2,320,256]{2,1,0:T(8,128)(2,1)} %bitcast.1), calls=%async_computation | async-start | bytes 655360 | tf_op jit(solution)/shard_map/all_to_all | solution.py:234
  15.6 15.8 %all-to-all-start.1 = ((bf16[32,8,512]{2,1,0:T(8,128)(2,1)}), bf16[32,8,512]{2,1,0:T(8,128)(2,1)S(1)}, u32[]{:S(2)}, u32[]{:S(2)}) async-start(bf16[32,8,512]{2,1,0:T(8,128)(2,1)} %bitcast.8), calls=%async_computation.1 | async-start | bytes 524288 | tf_op jit(solution)/shard_map/all_to_all | solution.py:261
  22.0 9.4 %copy-start = (s32[20]{0:T(128)S(1)}, s32[20]{0:T(128)}, u32[]{:S(2)}) copy-start(s32[20]{0:T(128)} %count_ref.3) | copy-start | bytes 244
  44.2 14.8 %all-to-all-start.2 = ((bf16[32,8,512]{2,1,0:T(8,128)(2,1)}), bf16[32,8,512]{2,1,0:T(8,128)(2,1)S(1)}, u32[]{:S(2)}, u32[]{:S(2)}) async-start(bf16[32,8,512]{2,1,0:T(8,128)(2,1)} %bitcast.9), calls=%async_computation.2 | async-start | bytes 524288 | tf_op jit(solution)/shard_map/all_to_all | solution.py:261
